TPU v7x, 32 devices: a whole 2x2x4 slice. The times are simulated.
32 devices in a mesh: replica: 8 (over z, core), tp: 4 (over y, x).
Axes of the slice: x: 2, y: 2, z: 4, core: 2. Of those that a mesh axis runs over, the one named last changes fastest.
Arguments:
- token_ids: int32 [128], replicated, may hold values from 0 to 8191
- embed_table: bfloat16 [8192, 8192], P('replica', 'tp'), may hold values from -6 to 6
- norm_gain: bfloat16 [8192], replicated, may hold values from 0.099609375 to 1.8984375
- w_query: bfloat16 [8192, 4096], P(('replica', 'tp')), may hold values from -0.0625 to 0.0625
- w_keyvalue: bfloat16 [8192, 2, 512], P(('replica', 'tp')), may hold values from -0.0625 to 0.0625
- key_cache: bfloat16 [512, 1024, 128], P(('replica', 'tp')), may hold values from -360 to 360
- value_cache: bfloat16 [512, 1024, 128], P(('replica', 'tp')), may hold values from -6 to 6
- cache_lengths: int32 [128], P('replica'), may hold values from 1 to 1024, as said below
Outputs:
- context: bfloat16 [512, 1024], P(('replica', 'tp'))
- query_weight_tp: bfloat16 [8192, 4096], P(None, 'tp')
- keyvalue_weight_tp: bfloat16 [8192, 2, 512], P(None, None, 'tp')
Inputs may be any that keep to these rules, and one draw needn't show every extreme that they name: `cache_lengths`: some sequence has exactly 1024 filled slots.
All inputs are finite; a program needn't handle non-finite values.
Results may differ from a plain program's by a relative error of at most 0.019.
The roundings to bfloat16 on the way count: a program that leaves them out, or rounds other values in their place, can miss the bound.
Values may be sent and summed in bfloat16 or wider, within the bound.
A program may use at most 128 MiB of HBM per device.

v0:
```python
import jax
import jax.numpy as jnp
from jax import lax
from jax.sharding import PartitionSpec as P


def attend(query, keys, values, key_new, value_new, lengths):
    scale = query.shape[-1] ** (-0.5)
    scores = jnp.einsum("rgd,rcd->rgc", query, keys, preferred_element_type=jnp.float32) * scale
    position = lax.broadcasted_iota(jnp.int32, scores.shape, 2)
    scores = jnp.where(position < lengths[:, None, None], scores, -jnp.inf)
    own = jnp.einsum("rgd,rd->rg", query, key_new, preferred_element_type=jnp.float32) * scale
    top = jnp.maximum(jnp.max(scores, axis=2), own)
    weights = jnp.exp(scores - top[:, :, None])
    own_weight = jnp.exp(own - top)
    total = jnp.sum(weights, axis=2) + own_weight
    weights = (weights / total[:, :, None]).astype(jnp.bfloat16)
    own_weight = (own_weight / total).astype(jnp.bfloat16)
    context = jnp.einsum("rgc,rcd->rgd", weights, values, preferred_element_type=jnp.float32)
    context = (
        context
        + own_weight.astype(jnp.float32)[:, :, None] * value_new.astype(jnp.float32)[:, None, :]
    )
    return context.astype(jnp.bfloat16)


def per_device(
    token_ids, embed_table, norm_gain, w_query, w_keyvalue, key_cache, value_cache, cache_lengths
):
    group_index = lax.axis_index("replica")
    tp_index = lax.axis_index("tp")
    vocab_rows, feature_cols = embed_table.shape
    batch = cache_lengths.shape[0]
    first_id = group_index * vocab_rows
    picked = token_ids - first_id
    columns = lax.broadcasted_iota(jnp.int32, (batch * lax.axis_size("replica"), vocab_rows), 1)
    onehot = (picked[:, None] == columns).astype(jnp.bfloat16)
    embedded = lax.psum_scatter(
        jnp.dot(onehot, embed_table, preferred_element_type=jnp.float32),
        "replica",
        scatter_dimension=0,
        tiled=True,
    ).astype(jnp.bfloat16)
    whole = lax.all_gather(embedded, "tp", axis=1, tiled=True)
    values32 = whole.astype(jnp.float32)
    mean_square = jnp.mean(values32 * values32, axis=1, keepdims=True)
    normed = (values32 * lax.rsqrt(mean_square + 1e-05) * norm_gain.astype(jnp.float32)).astype(
        jnp.bfloat16
    )
    width = normed.shape[1]
    query_rows = w_query.reshape(w_query.shape[0], 1, w_query.shape[1])
    query_mid, pair_mid = (
        lax.all_to_all(query_rows, "tp", split_axis=2, concat_axis=0, tiled=True),
        lax.all_to_all(w_keyvalue, "tp", split_axis=2, concat_axis=0, tiled=True),
    )
    flat_query = query_mid.reshape(query_mid.shape[0], query_mid.shape[2])
    pair_cols = pair_mid.shape[2]
    flat_pair = pair_mid.reshape(pair_mid.shape[0], 2 * pair_cols)
    query_full, pair_full = (
        lax.all_gather(flat_query, "replica", axis=0, tiled=True),
        lax.all_gather(flat_pair, "replica", axis=0, tiled=True),
    )
    query_acc = jnp.dot(normed, query_full, preferred_element_type=jnp.float32)
    pair_acc = jnp.dot(normed, pair_full, preferred_element_type=jnp.float32)
    query_local = query_acc.astype(jnp.bfloat16)
    pair_local = pair_acc.astype(jnp.bfloat16).reshape(batch, 2, pair_cols)
    query_heads, pair_heads = (
        lax.all_gather(query_local, "tp", axis=1, tiled=True),
        lax.all_gather(pair_local, "tp", axis=2, tiled=True),
    )
    head_size = key_cache.shape[2]
    kv_heads = pair_heads.shape[2] // head_size
    group = query_heads.shape[1] // (kv_heads * head_size)
    rows_here = key_cache.shape[0]
    first_row = tp_index * rows_here
    query_grouped = (
        query_heads.reshape(batch, kv_heads, group, head_size)
        .transpose(1, 0, 2, 3)
        .reshape(kv_heads * batch, group, head_size)
    )
    key_grouped = (
        pair_heads[:, 0]
        .reshape(batch, kv_heads, head_size)
        .transpose(1, 0, 2)
        .reshape(kv_heads * batch, head_size)
    )
    value_grouped = (
        pair_heads[:, 1]
        .reshape(batch, kv_heads, head_size)
        .transpose(1, 0, 2)
        .reshape(kv_heads * batch, head_size)
    )
    query_mine = lax.dynamic_slice_in_dim(query_grouped, first_row, rows_here, 0)
    key_mine = lax.dynamic_slice_in_dim(key_grouped, first_row, rows_here, 0)
    value_mine = lax.dynamic_slice_in_dim(value_grouped, first_row, rows_here, 0)
    sequence = (first_row + lax.broadcasted_iota(jnp.int32, (rows_here,), 0)) % batch
    matches = sequence[:, None] == lax.broadcasted_iota(jnp.int32, (rows_here, batch), 1)
    row_lengths = jnp.sum(jnp.where(matches, cache_lengths[None, :], 0), axis=1)
    context = attend(query_mine, key_cache, value_cache, key_mine, value_mine, row_lengths)
    context = context.reshape(rows_here, group * head_size)
    return (context, query_full, pair_full.reshape(width, 2, pair_cols))


def solution(mesh):
    return jax.shard_map(
        per_device,
        mesh=mesh,
        in_specs=(
            P(),
            P("replica", "tp"),
            P(),
            P(("replica", "tp"), None),
            P(("replica", "tp"), None, None),
            P(("replica", "tp"), None, None),
            P(("replica", "tp"), None, None),
            P("replica"),
        ),
        out_specs=(P(("replica", "tp"), None), P(None, "tp"), P(None, None, "tp")),
        check_vma=False,
    )
```

profile of v0, /device:TPU:0, one launch (start us, length us, event | category | flops | bytes accessed | tf_op | source)
XLA Modules:
  0.0 279.0 jit_solution(18418797829905342189)
XLA Ops:
  7.2 0.7 broadcast_subtract_fusion
  7.9 3.9 %fusion.6 = f32[128,2048]{1,0:T(8,128)} fusion(bf16[1024,2048]{1,0:T(8,128)(2,1)} %param.9, s32[128]{0:T(128)S(1)} %broadcast_subtract_fusion), kind=kOutput, calls=%fused_computation.17 | convolution fusion | flops 537001984 | bytes 5243392 | tf_op jit(solution)/shard_map/dot_general | solution.py:39
  11.9 0.0 all-gather.5.cloned.1.call-start
  11.9 1.0 copy.59
  12.9 13.5 %all_to_all.30 = bf16[256,2,512]{0,1,2:T(2,128)(2,1)S(1)} all-to-all(bf16[256,2,512]{0,1,2:T(2,128)(2,1)S(1)} %copy.59), channel_id=1, replica_groups=mesh['replica'=8,'tp'=4] {'tp'}, dimensions={2} | all-to-all | bytes 1048576 | tf_op jit(solution)/shard_map/all_to_all | solution.py:54
  26.5 0.6 copy.60
  27.1 0.9 copy.76
  28.0 0.0 all-gather.3.cloned.1.call-start
  28.1 7.1 %copy.56 = bf16[256,1,4096]{0,1,2:T(2,128)(2,1)} copy(bf16[256,1,4096]{2,0,1:T(8,128)(2,1)S(1)} %bitcast.52) | data formatting | bytes 4194304 | tf_op jit(solution)/shard_map/reshape | solution.py:51
  35.1 0.5 broadcast.60
  35.6 21.6 %reduce = bf16[4096,256]{1,0:T(8,128)(2,1)S(1)} reduce(bf16[4096,1,256]{2,1,0:T(2,128)(2,1)} %bitcast.48, bf16[]{:T(256)} %broadcast.60), dimensions={1}, to_apply=%bitcast.36.reduce_sub_computation | reduce | bytes 4194306
  57.2 2.1 reshape.81
  59.3 27.9 %all_to_all.31 = bf16[4,2,131072]{2,1,0:T(2,128)(2,1)S(1)} all-to-all(bf16[4,2,131072]{2,1,0:T(2,128)(2,1)} %reshape.81), channel_id=1, replica_groups=mesh['replica'=8,'tp'=4] {'tp'}, dimensions={0} | all-to-all | bytes 4194304 | tf_op jit(solution)/shard_map/all_to_all | solution.py:53
  87.1 3.3 %reshape.82 = bf16[4096,1,256]{2,1,0:T(2,128)(2,1)} reshape(bf16[4,2,131072]{2,1,0:T(2,128)(2,1)S(1)} %all_to_all.31) | data formatting | bytes 4194304
  90.4 2.6 copy.66
  93.0 2.4 copy.57
  95.5 0.2 select_reduce_fusion
  95.7 0.9 convert_element_type.34
  96.6 8.4 %all_gather.15 = bf16[16,8192]{1,0:T(8,128)(2,1)S(1)} all-gather(bf16[16,2048]{1,0:T(8,128)(2,1)S(1)} %convert_element_type.34), channel_id=1, replica_groups=mesh['replica'=8,'tp'=4] {'tp'}, dimensions={1}, use_global_device_ids=true | all-gather | bytes 327680 | tf_op jit(solution)/shard_map/all_gather | solution.py:44
  105.0 0.2 fusion.3
  105.2 3.8 %fusion.2 = bf16[2,2,8,128]{3,2,1,0:T(8,128)(2,1)S(1)} fusion(bf16[8192,256]{1,0:T(8,128)(2,1)} %all-gather.5.cloned.1.call-done, bf16[16,8192]{1,0:T(8,128)(2,1)S(1)} %all_gather.15, f32[8192]{0:T(1024)S(1)} %convert_element_type.36, f32[16]{0:T(128)S(1)} %add_rsqrt_fusion), kind=kOutput, calls=%fused_computation.6 | convolution fusion | flops 67637248 | bytes 4497472 | tf_op jit(solution)/shard_map/dot_general | solution.py:64
  109.0 7.4 %all_gather.19 = bf16[16,2,512]{2,0,1:T(8,128)(2,1)S(1)} all-gather(bf16[16,2,128]{2,0,1:T(8,128)(2,1)S(1)} %bitcast.65), channel_id=1, replica_groups=mesh['replica'=8,'tp'=4] {'tp'}, dimensions={2}, use_global_device_ids=true | all-gather | bytes 40960 | tf_op jit(solution)/shard_map/all_gather | solution.py:69
  116.5 7.0 %reshape.78 = bf16[8192,2,128]{2,1,0:T(2,128)(2,1)} reshape(bf16[8192,256]{1,0:T(8,128)(2,1)} %all-gather.5.cloned.1.call-done) | data formatting | bytes 8388608 | tf_op jit(solution)/shard_map/reshape | solution.py:101
  123.5 122.8 %all-gather.3.cloned.1.call-done = bf16[8192,1024]{1,0:T(8,128)(2,1)} async-done(((bf16[1024,1024]{1,0:T(8,128)(2,1)}), bf16[8192,1024]{1,0:T(8,128)(2,1)}) %all-gather.3.cloned.1.call-update) | async-done | bytes 16777232 | tf_op jit(solution)/shard_map/all_gather | solution.py:60
  246.3 8.2 %convolution_convert_fusion = bf16[16,1024]{1,0:T(8,128)(2,1)S(1)} fusion(bf16[8192,1024]{1,0:T(8,128)(2,1)} %all-gather.3.cloned.1.call-done, bf16[16,8192]{1,0:T(8,128)(2,1)S(1)} %all_gather.15, f32[8192]{0:T(1024)S(1)} %convert_element_type.36, f32[16]{0:T(128)S(1)} %add_rsqrt_fusion), kind=kOutput, calls=%fused_computation.4 | convolution fusion | flops 268976128 | bytes 17104960 | tf_op jit(solution)/shard_map/dot_general | solution.py:63
  254.5 8.7 %all_gather.17 = bf16[16,4096]{1,0:T(8,128)(2,1)S(1)} all-gather(bf16[16,1024]{1,0:T(8,128)(2,1)S(1)} %convolution_convert_fusion), channel_id=1, replica_groups=mesh['replica'=8,'tp'=4] {'tp'}, dimensions={1}, use_global_device_ids=true | all-gather | bytes 163840 | tf_op jit(solution)/shard_map/all_gather | solution.py:68
  263.3 0.1 fusion.13
  263.4 1.3 fusion.23
  264.7 0.2 fusion.7
  265.0 0.7 fusion.1
  265.7 0.6 copy.77
  266.3 6.2 %copy.80 = bf16[8192,1024]{1,0:T(8,128)(2,1)} copy(bf16[8192,1024]{1,0:T(8,128)(2,1)S(1)} %bitcast.47) | data formatting | bytes 33554432
  (42 shorter events, 0.3 us)
Async XLA Ops:
  7.2 4.8 %copy-start.3 = (bf16[256,2,512]{2,1,0:T(2,128)(2,1)S(1)}, bf16[256,2,512]{2,1,0:T(2,128)(2,1)}, u32[]{:S(2)}) copy-start(bf16[256,2,512]{2,1,0:T(2,128)(2,1)} %param.12) | copy-start | bytes 1572868
  7.2 88.5 %reduce-scatter.2.cloned.1.call-start = ((), (), s32[]{:S(2)}) async-start(), calls=%async_computation.3 | async-start | bytes 1179648 | tf_op jit(solution)/shard_map/reduce_scatter | solution.py:38
  11.8 16.2 %copy-start.2 = (bf16[256,4096]{1,0:T(8,128)(2,1)S(1)}, bf16[256,4096]{1,0:T(8,128)(2,1)}, u32[]{:S(2)}) copy-start(bf16[256,4096]{1,0:T(8,128)(2,1)} %param.11) | copy-start | bytes 6291460
  11.9 93.3 %all-gather.5.cloned.1.call-start = ((), (), s32[]{:S(2)}) async-start(), calls=%async_computation.5 | async-start | bytes 4718592 | tf_op jit(solution)/shard_map/all_gather | solution.py:61
  28.0 218.3 %all-gather.3.cloned.1.call-start = ((), (), s32[]{:S(2)}) async-start(), calls=%async_computation.4 | async-start | bytes 18874368 | tf_op jit(solution)/shard_map/all_gather | solution.py:60
  93.0 2.4 copy-start.4
  93.0 2.5 copy-start.5
  246.3 17.1 %copy-start.1 = (bf16[16,1024,128]{2,1,0:T(8,128)(2,1)S(1)}, bf16[16,1024,128]{2,1,0:T(8,128)(2,1)}, u32[]{:S(2)}) copy-start(bf16[16,1024,128]{2,1,0:T(8,128)(2,1)} %param.13) | copy-start | bytes 12582916
  246.3 20.0 %slice-start = ((s8[16777216]{0:T(1024)(128)(4,1)}), s8[4194304]{0:T(1024)(128)(4,1)S(1)}, s32[]{:S(2)}) async-start(s8[16777216]{0:T(1024)(128)(4,1)} %bitcast.46), calls=%async_computation.6 | async-start | bytes 8388608
  246.3 20.0 %slice-start.1 = ((s8[16777216]{0:T(1024)(128)(4,1)}), s8[4194304]{0:T(1024)(128)(4,1)S(1)}, s32[]{:S(2)}) async-start(s8[16777216]{0:T(1024)(128)(4,1)} %bitcast.46), calls=%async_computation.7 | async-start | bytes 8388608
  246.3 20.0 %slice-start.2 = ((s8[16777216]{0:T(1024)(128)(4,1)}), s8[4194304]{0:T(1024)(128)(4,1)S(1)}, s32[]{:S(2)}) async-start(s8[16777216]{0:T(1024)(128)(4,1)} %bitcast.46), calls=%async_computation.8 | async-start | bytes 8388608
  254.5 10.4 %copy-start = (bf16[16,1024,128]{2,1,0:T(8,128)(2,1)S(1)}, bf16[16,1024,128]{2,1,0:T(8,128)(2,1)}, u32[]{:S(2)}) copy-start(bf16[16,1024,128]{2,1,0:T(8,128)(2,1)} %param.14) | copy-start | bytes 12582916
  263.4 2.9 %slice-start.3 = ((s8[16777216]{0:T(1024)(128)(4,1)}), s8[4194304]{0:T(1024)(128)(4,1)S(1)}, s32[]{:S(2)}) async-start(s8[16777216]{0:T(1024)(128)(4,1)} %bitcast.46), calls=%async_computation.9 | async-start | bytes 8388608
Sparse Core Ops, SparseCore 0:
  12.0 35.2 reduce-scatter.1
  48.9 45.1 all-gather.4
  96.4 149.8 all-gather.2
where the time goes:
time: 280 us; the launch traced here: 279 us
  waiting for transfers between devices  123 us (44%)
  blocking collectives  65.9 us (24%)
  local copies, waits for them, and re-layouts  34.3 us (12%)
  other arithmetic  23.9 us (9%)
  matrix products  18 us (6%)
  between operations  14 us (5%)
    all_gather x1, waiting for transfers between devices, per_device(): lax.all_gather(flat_query, 'replica', axis=0, tiled=True)  123 us
    all_to_all x1, blocking collectives, per_device(): lax.all_to_all(query_rows, 'tp', split_axis=2, concat_axis=0, tiled=True)  27.9 us
    unnamed x2, other arithmetic  21.6 us
    unnamed x29, local copies, waits for them, and re-layouts  17.2 us
    all_to_all x1, blocking collectives, per_device(): lax.all_to_all(w_keyvalue, 'tp', split_axis=2, concat_axis=0, tiled=True)  13.5 us
    all_gather x1, blocking collectives, per_device(): lax.all_gather(query_local, 'tp', axis=1, tiled=True)  8.68 us
    all_gather x1, blocking collectives, per_device(): whole = lax.all_gather(embedded, 'tp', axis=1, tiled=True)  8.37 us
    dot_general x1, matrix products, per_device(): query_acc = jnp.dot(normed, query_full, preferred_element_type=jnp.float32)  8.22 us
  transfers between devices with their start and end apart: 3, of which 1 were waited for; matrix products, arithmetic and copies ran while one was open for 19% of the time, Pallas kernels for 0%

commit v1 on v0

--- a/solution.py
+++ b/solution.py
@@ -2,6 +2,10 @@
 import jax.numpy as jnp
 from jax import lax
 from jax.sharding import PartitionSpec as P
+
+matrix_attach = lambda inputs: jnp.concatenate(
+    jax.lax.all_to_all(jnp.stack(jnp.split(inputs, jax.lax.axis_size("tp"), 2), 0), "tp", 0, 0), 0
+)
 
 
 def attend(query, keys, values, key_new, value_new, lengths):
@@ -50,7 +54,7 @@
     width = normed.shape[1]
     query_rows = w_query.reshape(w_query.shape[0], 1, w_query.shape[1])
     query_mid, pair_mid = (
-        lax.all_to_all(query_rows, "tp", split_axis=2, concat_axis=0, tiled=True),
+        matrix_attach(query_rows),
         lax.all_to_all(w_keyvalue, "tp", split_axis=2, concat_axis=0, tiled=True),
     )
     flat_query = query_mid.reshape(query_mid.shape[0], query_mid.shape[2])

time: 280 us -> 280 us (level)
  waiting for transfers between devices: 123 us -> 163 us
  other arithmetic: 23.9 us -> 2.55 us
  local copies, waits for them, and re-layouts: 34.3 us -> 16.6 us
    all_gather x1, waiting for transfers between devices: 0.02 us -> 28.9 us  [per_device(): lax.all_gather(flat_pair, 'replica', axis=0, tiled=True)]
    unnamed x2 -> x1, other arithmetic: 21.6 us -> 0.01 us
    all_gather x1, waiting for transfers between devices: 123 us -> 133 us  [per_device(): lax.all_gather(flat_query, 'replica', axis=0, tiled=True)]
    unnamed x29 -> x25, local copies, waits for them, and re-layouts: 17.2 us -> 8.73 us
    reshape x1 -> x0, local copies, waits for them, and re-layouts: 7.06 us -> none  [per_device(): query_rows = w_query.reshape(w_query.shape[0], 1, w_query.shape[1])]
  transfers between devices with their start and end apart: 3 -> 3, of which waited for: 1 -> 2; matrix products, arithmetic and copies ran while one was open for 19% -> 5% of each run, Pallas kernels for 0% -> 0%
where the time goes in v1:
time: 280 us; the launch traced here: 279 us
  waiting for transfers between devices  163 us (58%)
  blocking collectives  66.1 us (24%)
  matrix products  17.2 us (6%)
  local copies, waits for them, and re-layouts  16.6 us (6%)
  between operations  14 us (5%)
    all_gather x1, waiting for transfers between devices, per_device(): lax.all_gather(flat_query, 'replica', axis=0, tiled=True)  133 us
    all_gather x1, waiting for transfers between devices, per_device(): lax.all_gather(flat_pair, 'replica', axis=0, tiled=True)  28.9 us
    all_to_all x1, blocking collectives, jax.lax.all_to_all(jnp.stack(jnp.split(inputs, jax.lax.axis_size('tp'), 2...  27.5 us
    all_to_all x1, blocking collectives, per_device(): lax.all_to_all(w_keyvalue, 'tp', split_axis=2, concat_axis=0, tiled=True)  13.5 us
    unnamed x25, local copies, waits for them, and re-layouts  8.73 us
    all_gather x1, blocking collectives, per_device(): lax.all_gather(query_local, 'tp', axis=1, tiled=True)  8.68 us
    all_gather x1, blocking collectives, per_device(): whole = lax.all_gather(embedded, 'tp', axis=1, tiled=True)  8.38 us
    dot_general x1, matrix products, per_device(): query_acc = jnp.dot(normed, query_full, preferred_element_type=jnp.float32)  8.22 us
  transfers between devices with their start and end apart: 3, of which 2 were waited for; matrix products, arithmetic and copies ran while one was open for 5% of the time, Pallas kernels for 0%

profile of v1, /device:TPU:0, one launch (start us, length us, event | category | flops | bytes accessed | tf_op | source)
XLA Modules:
  0.0 279.0 jit_solution(6646729180478213800)
XLA Ops:
  7.2 0.0 reduce-scatter.2.cloned.1.call-start
  7.2 0.7 broadcast_subtract_fusion
  7.9 3.9 %fusion.6 = f32[128,2048]{1,0:T(8,128)} fusion(bf16[1024,2048]{1,0:T(8,128)(2,1)} %param.9, s32[128]{0:T(128)S(1)} %broadcast_subtract_fusion), kind=kOutput, calls=%fused_computation.22 | convolution fusion | flops 537001984 | bytes 5243392 | tf_op jit(solution)/shard_map/dot_general | solution.py:43
  11.9 0.0 reduce-scatter.2.cloned.1.call-update
  11.9 0.0 all-gather.5.cloned.1.call-start
  11.9 1.0 copy.41
  12.9 13.5 %all_to_all.20 = bf16[256,2,512]{0,1,2:T(2,128)(2,1)S(1)} all-to-all(bf16[256,2,512]{0,1,2:T(2,128)(2,1)S(1)} %copy.41), channel_id=1, replica_groups=mesh['replica'=8,'tp'=4] {'tp'}, dimensions={2} | all-to-all | bytes 1048576 | tf_op jit(solution)/shard_map/all_to_all | solution.py:58
  26.5 0.6 copy.42
  27.1 0.9 copy.57
  28.0 0.0 all-gather.5.cloned.1.call-update
  28.0 0.0 all-gather.3.cloned.1.call-start
  28.0 0.2 slice_bitcast_fusion.3
  28.2 0.3 pad_maximum_fusion
  28.5 27.5 %all_to_all.21 = bf16[4,256,1,1024]{3,1,2,0:T(8,128)(2,1)} all-to-all(bf16[4,256,1,1024]{3,1,2,0:T(8,128)(2,1)S(1)} %pad_maximum_fusion), channel_id=1, replica_groups=mesh['replica'=8,'tp'=4] {'tp'}, dimensions={0} | all-to-all | bytes 4194304 | tf_op jit(solution)/shard_map/all_to_all | solution.py:7
  56.0 0.0 all-gather.3.cloned.1.call-update
  56.1 0.2 select_reduce_fusion
  56.3 0.9 convert_element_type.34
  57.2 8.4 %all_gather.15 = bf16[16,8192]{1,0:T(8,128)(2,1)S(1)} all-gather(bf16[16,2048]{1,0:T(8,128)(2,1)S(1)} %convert_element_type.34), channel_id=1, replica_groups=mesh['replica'=8,'tp'=4] {'tp'}, dimensions={1}, use_global_device_ids=true | all-gather | bytes 327680 | tf_op jit(solution)/shard_map/all_gather | solution.py:48
  65.6 0.2 fusion.3
  65.8 28.9 %all-gather.5.cloned.1.call-done = bf16[8192,256]{1,0:T(8,128)(2,1)} async-done(((bf16[1024,256]{1,0:T(8,128)(2,1)}), bf16[8192,256]{1,0:T(8,128)(2,1)}) %all-gather.5.cloned.1.call-update) | async-done | bytes 4194320 | tf_op jit(solution)/shard_map/all_gather | solution.py:65
  94.8 2.9 %fusion.2 = bf16[2,2,8,128]{3,2,1,0:T(8,128)(2,1)S(1)} fusion(bf16[8192,256]{1,0:T(8,128)(2,1)} %all-gather.5.cloned.1.call-done, bf16[16,8192]{1,0:T(8,128)(2,1)S(1)} %all_gather.15, f32[8192]{0:T(1024)S(1)} %convert_element_type.36, f32[16]{0:T(128)S(1)} %add_rsqrt_fusion), kind=kOutput, calls=%fused_computation.7 | convolution fusion | flops 67637248 | bytes 4497472 | tf_op jit(solution)/shard_map/dot_general | solution.py:68
  97.7 8.0 %all_gather.19 = bf16[16,2,512]{2,0,1:T(8,128)(2,1)S(1)} all-gather(bf16[16,2,128]{2,0,1:T(8,128)(2,1)S(1)} %bitcast.65), channel_id=1, replica_groups=mesh['replica'=8,'tp'=4] {'tp'}, dimensions={2}, use_global_device_ids=true | all-gather | bytes 40960 | tf_op jit(solution)/shard_map/all_gather | solution.py:73
  105.7 7.1 %reshape.73 = bf16[8192,2,128]{2,1,0:T(2,128)(2,1)} reshape(bf16[8192,256]{1,0:T(8,128)(2,1)} %all-gather.5.cloned.1.call-done) | data formatting | bytes 8388608 | tf_op jit(solution)/shard_map/reshape | solution.py:105
  112.8 133.5 %all-gather.3.cloned.1.call-done = bf16[8192,1024]{1,0:T(8,128)(2,1)} async-done(((bf16[1024,1024]{1,0:T(8,128)(2,1)}), bf16[8192,1024]{1,0:T(8,128)(2,1)}) %all-gather.3.cloned.1.call-update) | async-done | bytes 16777232 | tf_op jit(solution)/shard_map/all_gather | solution.py:64
  246.3 8.2 %convolution_convert_fusion = bf16[16,1024]{1,0:T(8,128)(2,1)S(1)} fusion(bf16[8192,1024]{1,0:T(8,128)(2,1)} %all-gather.3.cloned.1.call-done, bf16[16,8192]{1,0:T(8,128)(2,1)S(1)} %all_gather.15, f32[8192]{0:T(1024)S(1)} %convert_element_type.36, f32[16]{0:T(128)S(1)} %add_rsqrt_fusion), kind=kOutput, calls=%fused_computation.5 | convolution fusion | flops 268976128 | bytes 17104960 | tf_op jit(solution)/shard_map/dot_general | solution.py:67
  254.5 8.7 %all_gather.17 = bf16[16,4096]{1,0:T(8,128)(2,1)S(1)} all-gather(bf16[16,1024]{1,0:T(8,128)(2,1)S(1)} %convolution_convert_fusion), channel_id=1, replica_groups=mesh['replica'=8,'tp'=4] {'tp'}, dimensions={1}, use_global_device_ids=true | all-gather | bytes 163840 | tf_op jit(solution)/shard_map/all_gather | solution.py:72
  263.3 0.1 fusion.13
  263.4 1.3 fusion.23
  264.7 0.2 fusion.7
  265.0 0.7 fusion.1
  265.7 0.6 copy.58
  266.3 6.2 %copy.61 = bf16[8192,1024]{1,0:T(8,128)(2,1)} copy(bf16[8192,1024]{1,0:T(8,128)(2,1)S(1)} %bitcast.50) | data formatting | bytes 33554432
  (37 shorter events, 0.2 us)
Async XLA Ops:
  7.2 4.8 %copy-start.3 = (bf16[256,2,512]{2,1,0:T(2,128)(2,1)S(1)}, bf16[256,2,512]{2,1,0:T(2,128)(2,1)}, u32[]{:S(2)}) copy-start(bf16[256,2,512]{2,1,0:T(2,128)(2,1)} %param.12) | copy-start | bytes 1572868
  7.2 49.1 %reduce-scatter.2.cloned.1.call-start = ((), (), s32[]{:S(2)}) async-start(), calls=%async_computation.3 | async-start | bytes 1179648 | tf_op jit(solution)/shard_map/reduce_scatter | solution.py:42
  11.9 16.2 %copy-start.2 = (bf16[256,4096]{1,0:T(8,128)(2,1)S(1)}, bf16[256,4096]{1,0:T(8,128)(2,1)}, u32[]{:S(2)}) copy-start(bf16[256,4096]{1,0:T(8,128)(2,1)} %param.11) | copy-start | bytes 6291460
  11.9 82.9 %all-gather.5.cloned.1.call-start = ((), (), s32[]{:S(2)}) async-start(), calls=%async_computation.5 | async-start | bytes 4718592 | tf_op jit(solution)/shard_map/all_gather | solution.py:65
  28.0 218.3 %all-gather.3.cloned.1.call-start = ((), (), s32[]{:S(2)}) async-start(), calls=%async_computation.4 | async-start | bytes 18874368 | tf_op jit(solution)/shard_map/all_gather | solution.py:64
  28.5 27.6 %copy-start.4 = (bf16[8192]{0:T(1024)(128)(2,1)S(1)}, bf16[8192]{0:T(1024)(128)(2,1)}, u32[]{:S(2)}) copy-start(bf16[8192]{0:T(1024)(128)(2,1)} %param.10) | copy-start | bytes 49156
  28.5 27.6 %copy-start.5 = (s32[16]{0:T(128)S(1)}, s32[16]{0:T(128)}, u32[]{:S(2)}) copy-start(s32[16]{0:T(128)} %param.15) | copy-start | bytes 196
  246.3 17.1 %copy-start.1 = (bf16[16,1024,128]{2,1,0:T(8,128)(2,1)S(1)}, bf16[16,1024,128]{2,1,0:T(8,128)(2,1)}, u32[]{:S(2)}) copy-start(bf16[16,1024,128]{2,1,0:T(8,128)(2,1)} %param.13) | copy-start | bytes 12582916
  246.3 20.0 %slice-start = ((s8[16777216]{0:T(1024)(128)(4,1)}), s8[4194304]{0:T(1024)(128)(4,1)S(1)}, s32[]{:S(2)}) async-start(s8[16777216]{0:T(1024)(128)(4,1)} %bitcast.49), calls=%async_computation.6 | async-start | bytes 8388608
  246.3 20.0 %slice-start.1 = ((s8[16777216]{0:T(1024)(128)(4,1)}), s8[4194304]{0:T(1024)(128)(4,1)S(1)}, s32[]{:S(2)}) async-start(s8[16777216]{0:T(1024)(128)(4,1)} %bitcast.49), calls=%async_computation.7 | async-start | bytes 8388608
  246.3 20.0 %slice-start.2 = ((s8[16777216]{0:T(1024)(128)(4,1)}), s8[4194304]{0:T(1024)(128)(4,1)S(1)}, s32[]{:S(2)}) async-start(s8[16777216]{0:T(1024)(128)(4,1)} %bitcast.49), calls=%async_computation.8 | async-start | bytes 8388608
  254.5 10.4 %copy-start = (bf16[16,1024,128]{2,1,0:T(8,128)(2,1)S(1)}, bf16[16,1024,128]{2,1,0:T(8,128)(2,1)}, u32[]{:S(2)}) copy-start(bf16[16,1024,128]{2,1,0:T(8,128)(2,1)} %param.14) | copy-start | bytes 12582916
  263.4 2.9 %slice-start.3 = ((s8[16777216]{0:T(1024)(128)(4,1)}), s8[4194304]{0:T(1024)(128)(4,1)S(1)}, s32[]{:S(2)}) async-start(s8[16777216]{0:T(1024)(128)(4,1)} %bitcast.49), calls=%async_computation.9 | async-start | bytes 8388608
Sparse Core Ops, SparseCore 0:
  12.0 35.2 reduce-scatter.1
  49.5 45.1 all-gather.4
  96.4 149.8 all-gather.2
